TPU v7x, 256 devices: a whole 4x4x8 slice. The times are simulated.
256 devices in a mesh: row: 16 (over z, core), col: 16 (over y, x).
Axes of the slice: x: 4, y: 4, z: 8, core: 2. Of those that a mesh axis runs over, the one named last changes fastest.
Arguments:
- blocks: bfloat16 [256, 32, 256, 256], P('row', 'col'), may hold values from -0.0625 to 0.0625
- block_cols: int32 [256, 32], P('row', 'col'), may hold values from 0 to 48, as said below
- objective: float32 [196608], P(('col', 'row')), may hold values from -6 to 6
- lower_bound: float32 [196608], P(('col', 'row')), may hold values from -1 to -0.2
- upper_bound: float32 [196608], P(('col', 'row')), may hold values from 0.2 to 1
- right_side: float32 [65536], P(('row', 'col')), may hold values from -6 to 6
- primal_init: float32 [196608], P(('col', 'row')), may hold values from -0.2 to 0.2
- dual_init: float32 [65536], P(('row', 'col')), may hold values from 0 to 1
Outputs:
- primal_final: float32 [196608], P(('col', 'row'))
- dual_final: float32 [65536], P(('row', 'col'))
- step_norms: float32 [8, 2], replicated
Inputs may be any that keep to these rules, and one draw needn't show every extreme that they name: `block_cols`: entry j of a row block indexes column group j // 2; its live entries (below 48) are distinct within one row block and group, 48 marks an empty slot, and in every draw some row block has all 2 slots of some group live.
All inputs are finite; a program needn't handle non-finite values.
Results may differ from a plain program's by a relative error of at most 0.0015.
Values may be sent and summed in bfloat16 or wider, within the bound.
A program may use at most 64 MiB of HBM per device.

v0:
```python
import functools
import jax
import jax.numpy as jnp
from jax import lax
from jax.sharding import Mesh
from jax.sharding import PartitionSpec as P

ITERS = 8
ROW = ("row_0", "row_1")
COL = ("col_0", "col_1")
ROW_COL = ("row_0", "row_1", "col_0", "col_1")
COL_ROW = ("col_0", "col_1", "row_0", "row_1")
step_primal = 0.5
step_dual = 0.5


def gather_turned(arrays, axis, dims):
    turned = [jnp.moveaxis(a, dim, 0) for a, dim in zip(arrays, dims)]
    both = jnp.concatenate([t.reshape(len(t), -1) for t in turned], axis=1)
    whole, at, finished = (lax.all_gather(both, axis, axis=0, tiled=True), 0, [])
    for t, dim in zip(turned, dims):
        slab = whole[:, at : at + t[0].size].reshape(-1, *t.shape[1:])
        finished.append(jnp.moveaxis(slab, 0, dim))
        at += t[0].size
    return tuple(finished)


def over_pieces(array, axis):
    tiles = lax.all_gather(array, axis)
    return tiles.sum(axis=0)


def from_everyone(array, axis):
    count = lax.axis_size(axis)
    return lax.all_to_all(
        jnp.broadcast_to(array[None], (count, *array.shape)), axis, 0, 0, tiled=True
    )


def over_copies(array, axis):
    everything = from_everyone(array, axis)
    return jnp.sum(everything, axis=0)


def over_axes(array, axes):
    return functools.reduce(lax.psum, axes, array)


def per_device(
    blocks, block_cols, objective, lower_bound, upper_bound, right_side, primal_init, dual_init
):
    row_blocks = blocks.shape[0]
    slots = blocks.shape[1]
    width = blocks.shape[2]
    row_devices = lax.axis_size(ROW)
    col_devices = lax.axis_size(COL)
    primal_len = objective.shape[0]
    dual_len = right_side.shape[0]
    col_blocks = primal_len * row_devices // width
    primal_total = float(primal_len * row_devices * col_devices)
    dual_total = float(dual_len * row_devices * col_devices)
    flat_cols = block_cols.reshape(-1)
    chosen = flat_cols[:, None] == jnp.arange(col_blocks, dtype=jnp.int32)[None, :]
    chosen_half = chosen.astype(jnp.bfloat16)
    chosen_full = chosen.astype(jnp.float32)
    history = []
    primal_slab, objective_slab, lower_slab, upper_slab = gather_turned(
        (primal_init, objective, lower_bound, upper_bound), ROW, (0, 0, 0, 0)
    )
    dual_slab, right_slab = gather_turned((dual_init, right_side), COL, (0, 0))
    primal_offset = lax.axis_index(ROW) * primal_len
    dual_offset = lax.axis_index(COL) * dual_len
    for iteration in range(ITERS):
        dual_half = dual_slab.astype(jnp.bfloat16)
        dual_amount = dual_half.shape[0] // width
        products = jnp.einsum(
            "rsab,ra->rsb",
            blocks,
            dual_half.reshape(dual_amount, width),
            preferred_element_type=jnp.float32,
        ).reshape(dual_amount * slots, width)
        gradient = over_pieces(
            jnp.dot(
                chosen_full.T,
                products,
                precision=lax.Precision.HIGHEST,
                preferred_element_type=jnp.float32,
            ).reshape(-1),
            ROW,
        )
        primal_next = jnp.minimum(
            upper_slab,
            jnp.maximum(lower_slab, primal_slab - step_primal * (objective_slab - gradient)),
        )
        extrapolated = (2.0 * primal_next - primal_slab).astype(jnp.bfloat16)
        pick_amount = extrapolated.shape[0] // width
        picked = jnp.dot(
            chosen_half,
            extrapolated.reshape(pick_amount, width),
            preferred_element_type=jnp.float32,
        )
        shaped = picked.astype(jnp.bfloat16).reshape(row_blocks, slots, width)
        image_dual = over_copies(
            jnp.einsum("rsab,rsb->ra", blocks, shaped, preferred_element_type=jnp.float32).reshape(
                -1
            ),
            COL,
        )
        dual_next = jnp.maximum(dual_slab + step_dual * (right_slab - image_dual), 0.0)
        primal_step = lax.dynamic_slice_in_dim(
            primal_next - primal_slab, primal_offset, primal_len, 0
        )
        dual_step = lax.dynamic_slice_in_dim(dual_next - dual_slab, dual_offset, dual_len, 0)
        history.append(
            jnp.stack((jnp.sum(primal_step * primal_step), jnp.sum(dual_step * dual_step)))
        )
        primal_slab = primal_next
        dual_slab = dual_next
    primal_out = lax.dynamic_slice_in_dim(primal_slab, primal_offset, primal_len, 0)
    dual_out = lax.dynamic_slice_in_dim(dual_slab, dual_offset, dual_len, 0)
    stacked = jnp.stack(history)
    stacked = over_axes(stacked, ROW_COL)
    totals = jnp.array([primal_total, dual_total], jnp.float32)
    step_norms = jnp.sqrt(stacked / totals[None, :])
    return (primal_out, dual_out, step_norms)


def solution(mesh):
    split = Mesh(mesh.devices.reshape(8, 2, 4, 4), ("row_0", "row_1", "col_0", "col_1"))
    placed = (
        P(ROW, COL, None, None),
        P(ROW, COL),
        P(COL_ROW),
        P(COL_ROW),
        P(COL_ROW),
        P(ROW_COL),
        P(COL_ROW),
        P(ROW_COL),
    )
    return jax.shard_map(
        per_device,
        mesh=split,
        in_specs=placed,
        out_specs=(P(COL_ROW), P(ROW_COL), P()),
        check_vma=False,
    )
```

profile of v0, /device:TPU:32, one launch (start us, length us, event | category | flops | bytes accessed | tf_op | source)
XLA Modules:
  0.0 402.9 jit_solution(3310335284656649400)
XLA Ops:
  0.7 0.8 copy.34
  1.5 0.7 pad_maximum_fusion.1
  2.2 23.7 %all_gather.31 = f32[4096,2]{0,1:T(2,128)S(1)} all-gather(f32[256,2]{0,1:T(2,128)S(1)} %pad_maximum_fusion.1), channel_id=1, replica_groups=mesh['row_0'=8,'row_1'=2,'col_0'=4,'col_1'=4] {'col_0','col_1'}, dimensions={0}, use_global_device_ids=true | all-gather | bytes 34816 | tf_op jit(solution)/shard_map/all_gather | solution.py:20
  26.0 2.8 fusion.17
  29.3 20.0 %all-gather = f32[16,1,12288]{2,1,0:T(1,128)S(1)} all-gather(f32[1,1,12288]{2,1,0:T(1,128)S(1)} %reshape.329), channel_id=1, replica_groups=mesh['row_0'=8,'row_1'=2,'col_0'=4,'col_1'=4] {'row_0','row_1'}, dimensions={0}, use_global_device_ids=true | all-gather | bytes 835584 | tf_op jit(solution)/shard_map/all_gather | solution.py:29
  50.0 16.9 %all_gather.30 = f32[12288,4]{0,1:T(4,128)S(1)} all-gather(f32[768,4]{0,1:T(4,128)S(1)} %pad_maximum_fusion), channel_id=1, replica_groups=mesh['row_0'=8,'row_1'=2,'col_0'=4,'col_1'=4] {'row_0','row_1'}, dimensions={0}, use_global_device_ids=true | all-gather | bytes 208896 | tf_op jit(solution)/shard_map/all_gather | solution.py:20
  66.8 0.6 slice_reduce_fusion.3
  67.8 3.4 fusion.63
  71.2 0.9 broadcast_in_dim.59
  72.1 4.9 %all-to-all-start = ((f32[16,1,4096]{2,1,0:T(1,128)}), f32[16,1,4096]{2,1,0:T(1,128)S(1)}, u32[]{:S(2)}, u32[]{:S(2)}) async-start(f32[16,1,4096]{2,1,0:T(1,128)} %broadcast_in_dim.59), calls=%async_computation | async-start | bytes 524288 | tf_op jit(solution)/shard_map/all_to_all | solution.py:35
  77.0 9.2 %all-to-all-done = f32[16,1,4096]{2,1,0:T(1,128)S(1)} async-done(((f32[16,1,4096]{2,1,0:T(1,128)}), f32[16,1,4096]{2,1,0:T(1,128)S(1)}, u32[]{:S(2)}, u32[]{:S(2)}) %all-to-all-start) | async-done | bytes 262176 | tf_op jit(solution)/shard_map/all_to_all | solution.py:35
  86.4 2.8 fusion.15
  89.6 16.6 %all-gather.1 = f32[16,1,12288]{2,1,0:T(1,128)S(1)} all-gather(f32[1,1,12288]{2,1,0:T(1,128)S(1)} %reshape.331), channel_id=1, replica_groups=mesh['row_0'=8,'row_1'=2,'col_0'=4,'col_1'=4] {'row_0','row_1'}, dimensions={0}, use_global_device_ids=true | all-gather | bytes 835584 | tf_op jit(solution)/shard_map/all_gather | solution.py:29
  107.0 3.4 fusion.64
  110.6 12.1 %all_to_all.48 = f32[16,1,4096]{2,1,0:T(1,128)S(1)} all-to-all(f32[16,1,4096]{2,1,0:T(1,128)S(1)} %broadcast_in_dim.61), channel_id=1, replica_groups=mesh['row_0'=8,'row_1'=2,'col_0'=4,'col_1'=4] {'col_0','col_1'}, dimensions={0} | all-to-all | bytes 524288 | tf_op jit(solution)/shard_map/all_to_all | solution.py:35
  122.9 2.8 fusion.13
  126.2 18.0 %all-gather.2 = f32[16,1,12288]{2,1,0:T(1,128)S(1)} all-gather(f32[1,1,12288]{2,1,0:T(1,128)S(1)} %reshape.333), channel_id=1, replica_groups=mesh['row_0'=8,'row_1'=2,'col_0'=4,'col_1'=4] {'row_0','row_1'}, dimensions={0}, use_global_device_ids=true | all-gather | bytes 835584 | tf_op jit(solution)/shard_map/all_gather | solution.py:29
  144.9 3.4 fusion.65
  148.5 12.1 %all_to_all.49 = f32[16,1,4096]{2,1,0:T(1,128)S(1)} all-to-all(f32[16,1,4096]{2,1,0:T(1,128)S(1)} %broadcast_in_dim.63), channel_id=1, replica_groups=mesh['row_0'=8,'row_1'=2,'col_0'=4,'col_1'=4] {'col_0','col_1'}, dimensions={0} | all-to-all | bytes 524288 | tf_op jit(solution)/shard_map/all_to_all | solution.py:35
  160.8 2.8 fusion.11
  164.0 16.6 %all-gather.3 = f32[16,1,12288]{2,1,0:T(1,128)S(1)} all-gather(f32[1,1,12288]{2,1,0:T(1,128)S(1)} %reshape.335), channel_id=1, replica_groups=mesh['row_0'=8,'row_1'=2,'col_0'=4,'col_1'=4] {'row_0','row_1'}, dimensions={0}, use_global_device_ids=true | all-gather | bytes 835584 | tf_op jit(solution)/shard_map/all_gather | solution.py:29
  181.4 3.4 fusion.66
  184.8 0.9 broadcast_in_dim.65
  185.7 3.7 all-to-all-start.3
  189.5 9.2 %all-to-all-done.3 = f32[16,1,4096]{2,1,0:T(1,128)S(1)} async-done(((f32[16,1,4096]{2,1,0:T(1,128)}), f32[16,1,4096]{2,1,0:T(1,128)S(1)}, u32[]{:S(2)}, u32[]{:S(2)}) %all-to-all-start.3) | async-done | bytes 262176 | tf_op jit(solution)/shard_map/all_to_all | solution.py:35
  198.9 2.8 fusion.9
  202.2 18.0 %all-gather.4 = f32[16,1,12288]{2,1,0:T(1,128)S(1)} all-gather(f32[1,1,12288]{2,1,0:T(1,128)S(1)} %reshape.337), channel_id=1, replica_groups=mesh['row_0'=8,'row_1'=2,'col_0'=4,'col_1'=4] {'row_0','row_1'}, dimensions={0}, use_global_device_ids=true | all-gather | bytes 835584 | tf_op jit(solution)/shard_map/all_gather | solution.py:29
  220.9 3.4 fusion.67
  224.3 0.9 broadcast_in_dim.67
  225.2 3.5 all-to-all-start.4
  228.7 9.4 %all-to-all-done.4 = f32[16,1,4096]{2,1,0:T(1,128)S(1)} async-done(((f32[16,1,4096]{2,1,0:T(1,128)}), f32[16,1,4096]{2,1,0:T(1,128)S(1)}, u32[]{:S(2)}, u32[]{:S(2)}) %all-to-all-start.4) | async-done | bytes 262176 | tf_op jit(solution)/shard_map/all_to_all | solution.py:35
  238.4 2.8 fusion.7
  241.6 16.6 %all-gather.5 = f32[16,1,12288]{2,1,0:T(1,128)S(1)} all-gather(f32[1,1,12288]{2,1,0:T(1,128)S(1)} %reshape.339), channel_id=1, replica_groups=mesh['row_0'=8,'row_1'=2,'col_0'=4,'col_1'=4] {'row_0','row_1'}, dimensions={0}, use_global_device_ids=true | all-gather | bytes 835584 | tf_op jit(solution)/shard_map/all_gather | solution.py:29
  259.0 3.4 fusion.68
  262.4 0.9 broadcast_in_dim.69
  263.3 3.5 all-to-all-start.5
  266.9 9.4 %all-to-all-done.5 = f32[16,1,4096]{2,1,0:T(1,128)S(1)} async-done(((f32[16,1,4096]{2,1,0:T(1,128)}), f32[16,1,4096]{2,1,0:T(1,128)S(1)}, u32[]{:S(2)}, u32[]{:S(2)}) %all-to-all-start.5) | async-done | bytes 262176 | tf_op jit(solution)/shard_map/all_to_all | solution.py:35
  276.5 2.8 fusion.5
  279.7 18.0 %all-gather.6 = f32[16,1,12288]{2,1,0:T(1,128)S(1)} all-gather(f32[1,1,12288]{2,1,0:T(1,128)S(1)} %reshape.341), channel_id=1, replica_groups=mesh['row_0'=8,'row_1'=2,'col_0'=4,'col_1'=4] {'row_0','row_1'}, dimensions={0}, use_global_device_ids=true | all-gather | bytes 835584 | tf_op jit(solution)/shard_map/all_gather | solution.py:29
  298.4 3.4 fusion.69
  301.8 0.9 broadcast_in_dim.71
  302.7 3.5 all-to-all-start.6
  306.3 9.4 %all-to-all-done.6 = f32[16,1,4096]{2,1,0:T(1,128)S(1)} async-done(((f32[16,1,4096]{2,1,0:T(1,128)}), f32[16,1,4096]{2,1,0:T(1,128)S(1)}, u32[]{:S(2)}, u32[]{:S(2)}) %all-to-all-start.6) | async-done | bytes 262176 | tf_op jit(solution)/shard_map/all_to_all | solution.py:35
  315.9 2.8 fusion.3
  319.2 16.6 %all-gather.7 = f32[16,1,12288]{2,1,0:T(1,128)S(1)} all-gather(f32[1,1,12288]{2,1,0:T(1,128)S(1)} %reshape.343), channel_id=1, replica_groups=mesh['row_0'=8,'row_1'=2,'col_0'=4,'col_1'=4] {'row_0','row_1'}, dimensions={0}, use_global_device_ids=true | all-gather | bytes 835584 | tf_op jit(solution)/shard_map/all_gather | solution.py:29
  336.6 3.4 fusion.70
  340.0 0.9 broadcast_in_dim.73
  340.9 3.5 all-to-all-start.7
  344.4 1.4 multiply_reduce_fusion
  345.8 8.0 %all-to-all-done.7 = f32[16,1,4096]{2,1,0:T(1,128)S(1)} async-done(((f32[16,1,4096]{2,1,0:T(1,128)}), f32[16,1,4096]{2,1,0:T(1,128)S(1)}, u32[]{:S(2)}, u32[]{:S(2)}) %all-to-all-start.7) | async-done | bytes 262176 | tf_op jit(solution)/shard_map/all_to_all | solution.py:35
  354.0 1.3 multiply_reduce_fusion.7
  355.4 1.4 maximum_bitcast_fusion.7
  356.9 1.3 maximum_bitcast_fusion.6
  358.3 1.2 maximum_bitcast_fusion.5
  359.6 1.4 maximum_bitcast_fusion.4
  361.1 1.4 maximum_bitcast_fusion.3
  362.6 1.3 maximum_bitcast_fusion.2
  363.9 1.3 maximum_bitcast_fusion.1
  365.3 1.4 maximum_bitcast_fusion
  366.8 15.8 %psum.28 = f32[8,2]{0,1:T(2,128)S(1)} all-reduce(f32[8,2]{0,1:T(2,128)S(1)} %stack.131), channel_id=1, replica_groups=mesh['row_0'=8,'row_1'=2,'col_0'=4,'col_1'=4] {'row_0'}, use_global_device_ids=true, to_apply=%region_32.0 | all-reduce | flops 16 | bytes 128 | tf_op jit(solution)/shard_map/psum | solution.py:46
  382.6 2.5 psum.29
  385.1 8.5 %psum.30 = f32[8,2]{0,1:T(2,128)S(1)} all-reduce(f32[8,2]{0,1:T(2,128)S(1)} %psum.29), channel_id=1, replica_groups=mesh['row_0'=8,'row_1'=2,'col_0'=4,'col_1'=4] {'col_0'}, use_global_device_ids=true, to_apply=%region_34.0 | all-reduce | flops 16 | bytes 128 | tf_op jit(solution)/shard_map/psum | solution.py:46
  393.6 8.6 %psum.31 = f32[8,2]{0,1:T(2,128)S(1)} all-reduce(f32[8,2]{0,1:T(2,128)S(1)} %psum.30), channel_id=1, replica_groups=mesh['row_0'=8,'row_1'=2,'col_0'=4,'col_1'=4] {'col_1'}, use_global_device_ids=true, to_apply=%region_35.0 | all-reduce | flops 16 | bytes 128 | tf_op jit(solution)/shard_map/psum | solution.py:46
  402.2 0.6 multiply_sqrt_fusion
  (143 shorter events, 12.5 us)
Async XLA Ops:
  0.6 49.2 %copy-start = (f32[768]{0:T(1024)S(1)}, f32[768]{0:T(1024)}, u32[]{:S(2)}) copy-start(f32[768]{0:T(1024)} %param.15) | copy-start | bytes 9220
  0.6 49.2 %copy-start.1 = (f32[768]{0:T(1024)S(1)}, f32[768]{0:T(1024)}, u32[]{:S(2)}) copy-start(f32[768]{0:T(1024)} %param.11) | copy-start | bytes 9220
  0.7 49.2 %copy-start.2 = (f32[768]{0:T(1024)S(1)}, f32[768]{0:T(1024)}, u32[]{:S(2)}) copy-start(f32[768]{0:T(1024)} %param.12) | copy-start | bytes 9220
  0.7 49.3 %copy-start.3 = (f32[768]{0:T(1024)S(1)}, f32[768]{0:T(1024)}, u32[]{:S(2)}) copy-start(f32[768]{0:T(1024)} %param.13) | copy-start | bytes 9220
  72.1 14.1 %all-to-all-start = ((f32[16,1,4096]{2,1,0:T(1,128)}), f32[16,1,4096]{2,1,0:T(1,128)S(1)}, u32[]{:S(2)}, u32[]{:S(2)}) async-start(f32[16,1,4096]{2,1,0:T(1,128)} %broadcast_in_dim.59), calls=%async_computation | async-start | bytes 524288 | tf_op jit(solution)/shard_map/all_to_all | solution.py:35
  185.7 13.0 %all-to-all-start.3 = ((f32[16,1,4096]{2,1,0:T(1,128)}), f32[16,1,4096]{2,1,0:T(1,128)S(1)}, u32[]{:S(2)}, u32[]{:S(2)}) async-start(f32[16,1,4096]{2,1,0:T(1,128)} %broadcast_in_dim.65), calls=%async_computation.3 | async-start | bytes 524288 | tf_op jit(solution)/shard_map/all_to_all | solution.py:35
  225.2 13.0 %all-to-all-start.4 = ((f32[16,1,4096]{2,1,0:T(1,128)}), f32[16,1,4096]{2,1,0:T(1,128)S(1)}, u32[]{:S(2)}, u32[]{:S(2)}) async-start(f32[16,1,4096]{2,1,0:T(1,128)} %broadcast_in_dim.67), calls=%async_computation.4 | async-start | bytes 524288 | tf_op jit(solution)/shard_map/all_to_all | solution.py:35
  263.3 13.0 %all-to-all-start.5 = ((f32[16,1,4096]{2,1,0:T(1,128)}), f32[16,1,4096]{2,1,0:T(1,128)S(1)}, u32[]{:S(2)}, u32[]{:S(2)}) async-start(f32[16,1,4096]{2,1,0:T(1,128)} %broadcast_in_dim.69), calls=%async_computation.5 | async-start | bytes 524288 | tf_op jit(solution)/shard_map/all_to_all | solution.py:35
  302.7 13.0 %all-to-all-start.6 = ((f32[16,1,4096]{2,1,0:T(1,128)}), f32[16,1,4096]{2,1,0:T(1,128)S(1)}, u32[]{:S(2)}, u32[]{:S(2)}) async-start(f32[16,1,4096]{2,1,0:T(1,128)} %broadcast_in_dim.71), calls=%async_computation.6 | async-start | bytes 524288 | tf_op jit(solution)/shard_map/all_to_all | solution.py:35
  319.2 83.1 %copy-start.4 = (f32[2]{0:T(128)S(1)}, f32[2]{0:T(128)}, u32[]{:S(2)}) copy-start(f32[2]{0:T(128)} %constant.46) | copy-start | bytes 28
  340.9 13.0 %all-to-all-start.7 = ((f32[16,1,4096]{2,1,0:T(1,128)}), f32[16,1,4096]{2,1,0:T(1,128)S(1)}, u32[]{:S(2)}, u32[]{:S(2)}) async-start(f32[16,1,4096]{2,1,0:T(1,128)} %broadcast_in_dim.73), calls=%async_computation.7 | async-start | bytes 524288 | tf_op jit(solution)/shard_map/all_to_all | solution.py:35
where the time goes:
time: 405 us; the launch traced here: 403 us
  blocking collectives  241 us (60%)
  waiting for transfers between devices  54.6 us (13%)
  matrix products  53.5 us (13%)
  starting transfers between devices  22.8 us (6%)
  other arithmetic  20.5 us (5%)
  local copies, waits for them, and re-layouts  9.56 us (2%)
    all_gather x8, blocking collectives, over_pieces(): tiles = lax.all_gather(array, axis)  140 us
    all_to_all x6, waiting for transfers between devices, from_everyone(): lax.all_to_all(jnp.broadcast_to(array[None], (count, *array.shape)), axis...  54.6 us
    all_gather x2, blocking collectives, gather_turned(): lax.all_gather(both, axis, axis=0, tiled=True)  40.6 us
    psum x4, blocking collectives, over_axes(): return functools.reduce(lax.psum, axes, array)  35.4 us
    dot_general x8, matrix products, per_device(): jnp.einsum('rsab,rsb->ra', blocks, shaped, preferred_element_type=jnp.flo...  26.9 us
    all_to_all x2, blocking collectives, from_everyone(): lax.all_to_all(jnp.broadcast_to(array[None], (count, *array.shape)), axis...  24.2 us
    all_to_all x6, starting transfers between devices, from_everyone(): lax.all_to_all(jnp.broadcast_to(array[None], (count, *array.shape)), axis...  22.8 us
    dot_general x8, matrix products, per_device(): jnp.einsum('rsab,ra->rsb', blocks, dual_half.reshape(dual_amount, width),...  22.7 us
  transfers between devices with their start and end apart: 6, of which 6 were waited for; matrix products, arithmetic and copies ran while one was open for 0% of the time, Pallas kernels for 0%

commit v1 on v0

--- a/solution.py
+++ b/solution.py
@@ -14,10 +14,15 @@
 step_dual = 0.5
 
 
+def swapped_in(x, mesh_axis, dim):
+    stack = jnp.stack([x] * lax.axis_size(mesh_axis))
+    return jnp.concatenate(lax.all_to_all(stack, mesh_axis, 0, 0), axis=dim)
+
+
 def gather_turned(arrays, axis, dims):
     turned = [jnp.moveaxis(a, dim, 0) for a, dim in zip(arrays, dims)]
     both = jnp.concatenate([t.reshape(len(t), -1) for t in turned], axis=1)
-    whole, at, finished = (lax.all_gather(both, axis, axis=0, tiled=True), 0, [])
+    whole, at, finished = (swapped_in(both, axis, 0), 0, [])
     for t, dim in zip(turned, dims):
         slab = whole[:, at : at + t[0].size].reshape(-1, *t.shape[1:])
         finished.append(jnp.moveaxis(slab, 0, dim))

time: 405 us -> 386 us (0.953)
  blocking collectives: 241 us -> 199 us
  starting transfers between devices: 22.8 us -> 37 us
  waiting for transfers between devices: 54.6 us -> 58.9 us
    all_gather x2 -> x0, blocking collectives: 40.6 us -> none  [gather_turned(): lax.all_gather(both, axis, axis=0, tiled=True)]
    all_to_all x0 -> x2, starting transfers between devices: none -> 15.6 us  [swapped_in(): return jnp.concatenate(lax.all_to_all(stack, mesh_axis, 0, 0), axis=dim)]
  transfers between devices with their start and end apart: 6 -> 8, of which waited for: 6 -> 7; matrix products, arithmetic and copies ran while one was open for 0% -> 2% of each run, Pallas kernels for 0% -> 0%
where the time goes in v1:
time: 386 us; the launch traced here: 383 us
  blocking collectives  199 us (52%)
  waiting for transfers between devices  58.9 us (15%)
  matrix products  53.5 us (14%)
  starting transfers between devices  37 us (10%)
  other arithmetic  20.5 us (5%)
  local copies, waits for them, and re-layouts  13.6 us (4%)
    all_gather x8, blocking collectives, over_pieces(): tiles = lax.all_gather(array, axis)  140 us
    all_to_all x6, waiting for transfers between devices, from_everyone(): lax.all_to_all(jnp.broadcast_to(array[None], (count, *array.shape)), axis...  54.9 us
    psum x4, blocking collectives, over_axes(): return functools.reduce(lax.psum, axes, array)  34.9 us
    dot_general x8, matrix products, per_device(): jnp.einsum('rsab,rsb->ra', blocks, shaped, preferred_element_type=jnp.flo...  26.9 us
    all_to_all x2, blocking collectives, from_everyone(): lax.all_to_all(jnp.broadcast_to(array[None], (count, *array.shape)), axis...  24.2 us
    dot_general x8, matrix products, per_device(): jnp.einsum('rsab,ra->rsb', blocks, dual_half.reshape(dual_amount, width),...  22.7 us
    all_to_all x6, starting transfers between devices, from_everyone(): lax.all_to_all(jnp.broadcast_to(array[None], (count, *array.shape)), axis...  21.4 us
    all_to_all x2, starting transfers between devices, swapped_in(): return jnp.concatenate(lax.all_to_all(stack, mesh_axis, 0, 0), axis=dim)  15.6 us
  transfers between devices with their start and end apart: 8, of which 7 were waited for; matrix products, arithmetic and copies ran while one was open for 2% of the time, Pallas kernels for 0%

profile of v1, /device:TPU:32, one launch (start us, length us, event | category | flops | bytes accessed | tf_op | source)
XLA Modules:
  0.0 383.3 jit_solution(743928312672725123)
XLA Ops:
  0.6 0.7 pad_maximum_fusion.1
  1.9 7.0 %all-to-all-start.1 = ((f32[16,256,2]{1,2,0:T(2,128)}), f32[16,256,2]{1,2,0:T(2,128)S(1)}, u32[]{:S(2)}, u32[]{:S(2)}) async-start(f32[16,256,2]{1,2,0:T(2,128)} %stack.138), calls=%async_computation.1 | async-start | bytes 65536 | tf_op jit(solution)/shard_map/all_to_all | solution.py:19
  11.8 0.8 copy.34
  12.6 4.0 %all-to-all-done.1 = f32[16,256,2]{1,2,0:T(2,128)S(1)} async-done(((f32[16,256,2]{1,2,0:T(2,128)}), f32[16,256,2]{1,2,0:T(2,128)S(1)}, u32[]{:S(2)}, u32[]{:S(2)}) %all-to-all-start.1) | async-done | bytes 32800 | tf_op jit(solution)/shard_map/all_to_all | solution.py:19
  16.6 0.7 stack.137
  17.3 8.6 %all-to-all-start = ((f32[16,768,4]{1,2,0:T(4,128)}), f32[16,768,4]{1,2,0:T(4,128)S(1)}, u32[]{:S(2)}, u32[]{:S(2)}) async-start(f32[16,768,4]{1,2,0:T(4,128)} %stack.137), calls=%async_computation | async-start | bytes 393216 | tf_op jit(solution)/shard_map/all_to_all | solution.py:19
  26.0 2.8 fusion.17
  29.2 17.9 %all-gather = f32[16,1,12288]{2,1,0:T(1,128)S(1)} all-gather(f32[1,1,12288]{2,1,0:T(1,128)S(1)} %reshape.341), channel_id=1, replica_groups=mesh['row_0'=8,'row_1'=2,'col_0'=4,'col_1'=4] {'row_0','row_1'}, dimensions={0}, use_global_device_ids=true | all-gather | bytes 835584 | tf_op jit(solution)/shard_map/all_gather | solution.py:34
  48.6 3.4 fusion.63
  52.0 0.9 broadcast_in_dim.59
  52.9 3.5 all-to-all-start.2
  56.4 9.4 %all-to-all-done.2 = f32[16,1,4096]{2,1,0:T(1,128)S(1)} async-done(((f32[16,1,4096]{2,1,0:T(1,128)}), f32[16,1,4096]{2,1,0:T(1,128)S(1)}, u32[]{:S(2)}, u32[]{:S(2)}) %all-to-all-start.2) | async-done | bytes 262176 | tf_op jit(solution)/shard_map/all_to_all | solution.py:40
  66.1 2.8 fusion.15
  69.3 17.9 %all-gather.1 = f32[16,1,12288]{2,1,0:T(1,128)S(1)} all-gather(f32[1,1,12288]{2,1,0:T(1,128)S(1)} %reshape.343), channel_id=1, replica_groups=mesh['row_0'=8,'row_1'=2,'col_0'=4,'col_1'=4] {'row_0','row_1'}, dimensions={0}, use_global_device_ids=true | all-gather | bytes 835584 | tf_op jit(solution)/shard_map/all_gather | solution.py:34
  88.0 3.4 fusion.64
  91.6 12.1 %all_to_all.58 = f32[16,1,4096]{2,1,0:T(1,128)S(1)} all-to-all(f32[16,1,4096]{2,1,0:T(1,128)S(1)} %broadcast_in_dim.61), channel_id=1, replica_groups=mesh['row_0'=8,'row_1'=2,'col_0'=4,'col_1'=4] {'col_0','col_1'}, dimensions={0} | all-to-all | bytes 524288 | tf_op jit(solution)/shard_map/all_to_all | solution.py:40
  103.9 2.8 fusion.13
  107.2 17.4 %all-gather.2 = f32[16,1,12288]{2,1,0:T(1,128)S(1)} all-gather(f32[1,1,12288]{2,1,0:T(1,128)S(1)} %reshape.345), channel_id=1, replica_groups=mesh['row_0'=8,'row_1'=2,'col_0'=4,'col_1'=4] {'row_0','row_1'}, dimensions={0}, use_global_device_ids=true | all-gather | bytes 835584 | tf_op jit(solution)/shard_map/all_gather | solution.py:34
  125.3 3.4 fusion.65
  128.9 12.1 %all_to_all.59 = f32[16,1,4096]{2,1,0:T(1,128)S(1)} all-to-all(f32[16,1,4096]{2,1,0:T(1,128)S(1)} %broadcast_in_dim.63), channel_id=1, replica_groups=mesh['row_0'=8,'row_1'=2,'col_0'=4,'col_1'=4] {'col_0','col_1'}, dimensions={0} | all-to-all | bytes 524288 | tf_op jit(solution)/shard_map/all_to_all | solution.py:40
  141.2 2.8 fusion.11
  144.5 17.2 %all-gather.3 = f32[16,1,12288]{2,1,0:T(1,128)S(1)} all-gather(f32[1,1,12288]{2,1,0:T(1,128)S(1)} %reshape.347), channel_id=1, replica_groups=mesh['row_0'=8,'row_1'=2,'col_0'=4,'col_1'=4] {'row_0','row_1'}, dimensions={0}, use_global_device_ids=true | all-gather | bytes 835584 | tf_op jit(solution)/shard_map/all_gather | solution.py:34
  162.4 3.4 fusion.66
  165.8 0.9 broadcast_in_dim.65
  166.7 3.7 all-to-all-start.5
  170.4 9.2 %all-to-all-done.5 = f32[16,1,4096]{2,1,0:T(1,128)S(1)} async-done(((f32[16,1,4096]{2,1,0:T(1,128)}), f32[16,1,4096]{2,1,0:T(1,128)S(1)}, u32[]{:S(2)}, u32[]{:S(2)}) %all-to-all-start.5) | async-done | bytes 262176 | tf_op jit(solution)/shard_map/all_to_all | solution.py:40
  179.9 2.8 fusion.9
  183.1 17.4 %all-gather.4 = f32[16,1,12288]{2,1,0:T(1,128)S(1)} all-gather(f32[1,1,12288]{2,1,0:T(1,128)S(1)} %reshape.349), channel_id=1, replica_groups=mesh['row_0'=8,'row_1'=2,'col_0'=4,'col_1'=4] {'row_0','row_1'}, dimensions={0}, use_global_device_ids=true | all-gather | bytes 835584 | tf_op jit(solution)/shard_map/all_gather | solution.py:34
  201.3 3.4 fusion.67
  204.7 0.9 broadcast_in_dim.67
  205.6 3.5 all-to-all-start.6
  209.2 9.4 %all-to-all-done.6 = f32[16,1,4096]{2,1,0:T(1,128)S(1)} async-done(((f32[16,1,4096]{2,1,0:T(1,128)}), f32[16,1,4096]{2,1,0:T(1,128)S(1)}, u32[]{:S(2)}, u32[]{:S(2)}) %all-to-all-start.6) | async-done | bytes 262176 | tf_op jit(solution)/shard_map/all_to_all | solution.py:40
  218.8 2.8 fusion.7
  222.0 17.2 %all-gather.5 = f32[16,1,12288]{2,1,0:T(1,128)S(1)} all-gather(f32[1,1,12288]{2,1,0:T(1,128)S(1)} %reshape.351), channel_id=1, replica_groups=mesh['row_0'=8,'row_1'=2,'col_0'=4,'col_1'=4] {'row_0','row_1'}, dimensions={0}, use_global_device_ids=true | all-gather | bytes 835584 | tf_op jit(solution)/shard_map/all_gather | solution.py:34
  239.9 3.4 fusion.68
  243.3 0.9 broadcast_in_dim.69
  244.2 3.5 all-to-all-start.7
  247.8 9.4 %all-to-all-done.7 = f32[16,1,4096]{2,1,0:T(1,128)S(1)} async-done(((f32[16,1,4096]{2,1,0:T(1,128)}), f32[16,1,4096]{2,1,0:T(1,128)S(1)}, u32[]{:S(2)}, u32[]{:S(2)}) %all-to-all-start.7) | async-done | bytes 262176 | tf_op jit(solution)/shard_map/all_to_all | solution.py:40
  257.4 2.8 fusion.5
  260.7 17.4 %all-gather.6 = f32[16,1,12288]{2,1,0:T(1,128)S(1)} all-gather(f32[1,1,12288]{2,1,0:T(1,128)S(1)} %reshape.353), channel_id=1, replica_groups=mesh['row_0'=8,'row_1'=2,'col_0'=4,'col_1'=4] {'row_0','row_1'}, dimensions={0}, use_global_device_ids=true | all-gather | bytes 835584 | tf_op jit(solution)/shard_map/all_gather | solution.py:34
  278.9 3.4 fusion.69
  282.3 0.9 broadcast_in_dim.71
  283.2 3.5 all-to-all-start.8
  286.7 9.4 %all-to-all-done.8 = f32[16,1,4096]{2,1,0:T(1,128)S(1)} async-done(((f32[16,1,4096]{2,1,0:T(1,128)}), f32[16,1,4096]{2,1,0:T(1,128)S(1)}, u32[]{:S(2)}, u32[]{:S(2)}) %all-to-all-start.8) | async-done | bytes 262176 | tf_op jit(solution)/shard_map/all_to_all | solution.py:40
  296.3 2.8 fusion.3
  299.6 17.2 %all-gather.7 = f32[16,1,12288]{2,1,0:T(1,128)S(1)} all-gather(f32[1,1,12288]{2,1,0:T(1,128)S(1)} %reshape.355), channel_id=1, replica_groups=mesh['row_0'=8,'row_1'=2,'col_0'=4,'col_1'=4] {'row_0','row_1'}, dimensions={0}, use_global_device_ids=true | all-gather | bytes 835584 | tf_op jit(solution)/shard_map/all_gather | solution.py:34
  317.5 3.4 fusion.70
  320.9 0.9 broadcast_in_dim.73
  321.8 3.5 all-to-all-start.9
  325.4 1.4 multiply_reduce_fusion
  326.8 8.0 %all-to-all-done.9 = f32[16,1,4096]{2,1,0:T(1,128)S(1)} async-done(((f32[16,1,4096]{2,1,0:T(1,128)}), f32[16,1,4096]{2,1,0:T(1,128)S(1)}, u32[]{:S(2)}, u32[]{:S(2)}) %all-to-all-start.9) | async-done | bytes 262176 | tf_op jit(solution)/shard_map/all_to_all | solution.py:40
  335.0 1.3 multiply_reduce_fusion.7
  336.4 1.4 maximum_bitcast_fusion.7
  337.9 1.3 maximum_bitcast_fusion.6
  339.2 1.2 maximum_bitcast_fusion.5
  340.6 1.4 maximum_bitcast_fusion.4
  342.0 1.4 maximum_bitcast_fusion.3
  343.5 1.3 maximum_bitcast_fusion.2
  344.9 1.3 maximum_bitcast_fusion.1
  346.2 1.4 maximum_bitcast_fusion
  347.8 15.3 %psum.28 = f32[8,2]{0,1:T(2,128)S(1)} all-reduce(f32[8,2]{0,1:T(2,128)S(1)} %stack.171), channel_id=1, replica_groups=mesh['row_0'=8,'row_1'=2,'col_0'=4,'col_1'=4] {'row_0'}, use_global_device_ids=true, to_apply=%region_32.0 | all-reduce | flops 16 | bytes 128 | tf_op jit(solution)/shard_map/psum | solution.py:51
  363.1 2.5 psum.29
  365.5 8.5 %psum.30 = f32[8,2]{0,1:T(2,128)S(1)} all-reduce(f32[8,2]{0,1:T(2,128)S(1)} %psum.29), channel_id=1, replica_groups=mesh['row_0'=8,'row_1'=2,'col_0'=4,'col_1'=4] {'col_0'}, use_global_device_ids=true, to_apply=%region_34.0 | all-reduce | flops 16 | bytes 128 | tf_op jit(solution)/shard_map/psum | solution.py:51
  374.1 8.6 %psum.31 = f32[8,2]{0,1:T(2,128)S(1)} all-reduce(f32[8,2]{0,1:T(2,128)S(1)} %psum.30), channel_id=1, replica_groups=mesh['row_0'=8,'row_1'=2,'col_0'=4,'col_1'=4] {'col_1'}, use_global_device_ids=true, to_apply=%region_35.0 | all-reduce | flops 16 | bytes 128 | tf_op jit(solution)/shard_map/psum | solution.py:51
  (139 shorter events, 17.0 us)
Async XLA Ops:
  1.9 14.6 %all-to-all-start.1 = ((f32[16,256,2]{1,2,0:T(2,128)}), f32[16,256,2]{1,2,0:T(2,128)S(1)}, u32[]{:S(2)}, u32[]{:S(2)}) async-start(f32[16,256,2]{1,2,0:T(2,128)} %stack.138), calls=%async_computation.1 | async-start | bytes 65536 | tf_op jit(solution)/shard_map/all_to_all | solution.py:19
  17.3 30.4 %all-to-all-start = ((f32[16,768,4]{1,2,0:T(4,128)}), f32[16,768,4]{1,2,0:T(4,128)S(1)}, u32[]{:S(2)}, u32[]{:S(2)}) async-start(f32[16,768,4]{1,2,0:T(4,128)} %stack.137), calls=%async_computation | async-start | bytes 393216 | tf_op jit(solution)/shard_map/all_to_all | solution.py:19
  52.9 13.0 %all-to-all-start.2 = ((f32[16,1,4096]{2,1,0:T(1,128)}), f32[16,1,4096]{2,1,0:T(1,128)S(1)}, u32[]{:S(2)}, u32[]{:S(2)}) async-start(f32[16,1,4096]{2,1,0:T(1,128)} %broadcast_in_dim.59), calls=%async_computation.2 | async-start | bytes 524288 | tf_op jit(solution)/shard_map/all_to_all | solution.py:40
  166.7 13.0 %all-to-all-start.5 = ((f32[16,1,4096]{2,1,0:T(1,128)}), f32[16,1,4096]{2,1,0:T(1,128)S(1)}, u32[]{:S(2)}, u32[]{:S(2)}) async-start(f32[16,1,4096]{2,1,0:T(1,128)} %broadcast_in_dim.65), calls=%async_computation.5 | async-start | bytes 524288 | tf_op jit(solution)/shard_map/all_to_all | solution.py:40
  205.6 13.0 %all-to-all-start.6 = ((f32[16,1,4096]{2,1,0:T(1,128)}), f32[16,1,4096]{2,1,0:T(1,128)S(1)}, u32[]{:S(2)}, u32[]{:S(2)}) async-start(f32[16,1,4096]{2,1,0:T(1,128)} %broadcast_in_dim.67), calls=%async_computation.6 | async-start | bytes 524288 | tf_op jit(solution)/shard_map/all_to_all | solution.py:40
  244.2 13.0 %all-to-all-start.7 = ((f32[16,1,4096]{2,1,0:T(1,128)}), f32[16,1,4096]{2,1,0:T(1,128)S(1)}, u32[]{:S(2)}, u32[]{:S(2)}) async-start(f32[16,1,4096]{2,1,0:T(1,128)} %broadcast_in_dim.69), calls=%async_computation.7 | async-start | bytes 524288 | tf_op jit(solution)/shard_map/all_to_all | solution.py:40
  283.2 13.0 %all-to-all-start.8 = ((f32[16,1,4096]{2,1,0:T(1,128)}), f32[16,1,4096]{2,1,0:T(1,128)S(1)}, u32[]{:S(2)}, u32[]{:S(2)}) async-start(f32[16,1,4096]{2,1,0:T(1,128)} %broadcast_in_dim.71), calls=%async_computation.8 | async-start | bytes 524288 | tf_op jit(solution)/shard_map/all_to_all | solution.py:40
  299.6 83.1 %copy-start = (f32[2]{0:T(128)S(1)}, f32[2]{0:T(128)}, u32[]{:S(2)}) copy-start(f32[2]{0:T(128)} %constant.46) | copy-start | bytes 28
  321.8 13.0 %all-to-all-start.9 = ((f32[16,1,4096]{2,1,0:T(1,128)}), f32[16,1,4096]{2,1,0:T(1,128)S(1)}, u32[]{:S(2)}, u32[]{:S(2)}) async-start(f32[16,1,4096]{2,1,0:T(1,128)} %broadcast_in_dim.73), calls=%async_computation.9 | async-start | bytes 524288 | tf_op jit(solution)/shard_map/all_to_all | solution.py:40
